TPU v7x, 32 devices: a whole 2x2x4 slice. The times are simulated.
32 devices in a mesh: gx: 8 (over z, x), gy: 4 (over y, core).
Axes of the slice: x: 2, y: 2, z: 4, core: 2. Of those that a mesh axis runs over, the one named last changes fastest.
Arguments:
- pressure: float32 [10, 512, 2048], P(None, 'gx', 'gy'), may hold values from -6 to 6
- pressure_old: float32 [10, 512, 2048], P(None, 'gx', 'gy'), may hold values from -6 to 6
- conductivity: float32 [10, 512, 2048], P(None, 'gx', 'gy'), may hold values from 0.1 to 1
- porosity: float32 [10, 512, 2048], P(None, 'gx', 'gy'), may hold values from 2 to 8
- recharge: float32 [512, 2048], P('gx', 'gy'), may hold values from -6 to 6
- active: int32 [512, 2048], P('gx', 'gy'), may hold values from 0 to 1, as said below
Outputs:
- final_pressure: float32 [10, 512, 2048], P(None, 'gx', 'gy')
- linear_residual: float32 [10, 512, 2048], P(None, 'gx', 'gy')
Inputs may be any that keep to these rules, and one draw needn't show every extreme that they name: `active`: 1 marks a land column, 0 an ocean column.
All inputs are finite; a program needn't handle non-finite values.
Results may differ from a plain program's by a relative error of at most 0.0003.
Values sent between devices are 32-bit elements; how exact they have to be, the bound alone decides.
A program may use at most 128 MiB of HBM per device.

v0:
```python
import jax
import jax.numpy as jnp
from jax import lax
from jax.sharding import PartitionSpec as P

NEWTON = 2


residual_sat = 0.1
vertical_factor = 2.0
epsilon = 1e-06


def padded(cells, sides, width):
    for axis, dim in sides:
        count = lax.axis_size(axis)
        ends = count - 1
        head = lax.slice_in_dim(cells, 0, width, axis=dim)
        tail = lax.slice_in_dim(cells, cells.shape[dim] - width, cells.shape[dim], axis=dim)
        cells = jnp.concatenate(
            [
                lax.ppermute(tail, axis, [(i, (i + 1) % count) for i in range(ends)]),
                cells,
                lax.ppermute(head, axis, [((i + 1) % count, i) for i in range(ends)]),
            ],
            axis=dim,
        )
    return cells


def interior(array):
    return array[:, 1:-1, 1:-1]


def saturation(values):
    return residual_sat + (1.0 - residual_sat) * jax.nn.sigmoid(values)


def sat_slope(values):
    sigma = jax.nn.sigmoid(values)
    return (1.0 - residual_sat) * sigma * (1.0 - sigma)


def face_pair(press_low, press_high, cond_low, cond_high, act_low, act_high, factor, gravity):
    transmit = 0.5 * factor * (cond_low + cond_high) * act_low * act_high
    sig_low = jax.nn.sigmoid(press_low)
    sig_high = jax.nn.sigmoid(press_high)
    mobility = 0.5 * (sig_low * sig_low + sig_high * sig_high)
    head_drop = press_low - press_high + gravity
    coef_low = transmit * (mobility + sig_low * sig_low * (1.0 - sig_low) * head_drop)
    coef_high = transmit * (sig_high * sig_high * (1.0 - sig_high) * head_drop - mobility)
    return (coef_low, coef_high, transmit * mobility * head_drop)


def coefficients(pressure, conduct, active):
    across_x = face_pair(
        pressure[:, :-1, 1:-1],
        pressure[:, 1:, 1:-1],
        conduct[:, :-1, 1:-1],
        conduct[:, 1:, 1:-1],
        active[:, :-1, 1:-1],
        active[:, 1:, 1:-1],
        1.0,
        0.0,
    )
    across_y = face_pair(
        pressure[:, 1:-1, :-1],
        pressure[:, 1:-1, 1:],
        conduct[:, 1:-1, :-1],
        conduct[:, 1:-1, 1:],
        active[:, 1:-1, :-1],
        active[:, 1:-1, 1:],
        1.0,
        0.0,
    )
    inner_p = interior(pressure)
    inner_k = interior(conduct)
    inner_a = interior(active)
    across_z = face_pair(
        inner_p[:-1],
        inner_p[1:],
        inner_k[:-1],
        inner_k[1:],
        inner_a[:-1],
        inner_a[1:],
        vertical_factor,
        -1.0,
    )
    return (across_x, across_y, across_z)


def outflow(flow_x, flow_y, flow_z):
    total = flow_x[:, 1:] - flow_x[:, :-1] + flow_y[:, :, 1:] - flow_y[:, :, :-1]
    zeros = jnp.zeros_like(flow_z[:1])
    return total + jnp.concatenate([flow_z, zeros], 0) - jnp.concatenate([zeros, flow_z], 0)


def jacobian_apply(vector, faces, diagonal, active):
    x_low, x_high, x_flow = faces[0]
    y_low, y_high, y_flow = faces[1]
    z_low, z_high, z_flow = faces[2]
    flow_x = x_low * vector[:, :-1, 1:-1] + x_high * vector[:, 1:, 1:-1]
    flow_y = y_low * vector[:, 1:-1, :-1] + y_high * vector[:, 1:-1, 1:]
    center = interior(vector)
    flow_z = z_low * center[:-1] + z_high * center[1:]
    return active * (diagonal * center + outflow(flow_x, flow_y, flow_z)) + (1.0 - active) * center


def newton_residual(pressure, faces, pressure_old, porosity, recharge, active):
    center = interior(pressure)
    storage = porosity * (saturation(center) - saturation(pressure_old))
    inflow = jnp.concatenate([jnp.zeros_like(center[:-1]), recharge[None]], 0)
    flows = outflow(faces[0][2], faces[1][2], faces[2][2])
    return active * (storage - inflow + flows) + (1.0 - active) * center


def least_squares(first_norm, entry_one, entry_two, entry_three, entry_four, entry_five):
    radius = jnp.sqrt(entry_one * entry_one + entry_two * entry_two)
    cosine = entry_one / radius
    sine = entry_two / radius
    top_right = cosine * entry_three + sine * entry_four
    lower = cosine * entry_four - sine * entry_three
    weight_two = -lower * sine * first_norm / (lower * lower + entry_five * entry_five)
    weight_one = (cosine * first_norm - top_right * weight_two) / radius
    return (weight_one, weight_two)


def body(pressure, pressure_old, conductivity, porosity, recharge, active):
    layers = pressure.shape[0]
    active_flat = active.astype(jnp.float32)
    active_cells = jnp.broadcast_to(active_flat[None], pressure.shape)
    stacked = jnp.concatenate([conductivity, active_flat[None]], 0)
    widened = padded(stacked, (("gx", 1), ("gy", 2)), 1)
    cond_ext = widened[:layers]
    act_ext = jnp.broadcast_to(widened[layers][None], cond_ext.shape)
    current = pressure
    leftover = jnp.zeros_like(pressure)
    for newton_index in range(NEWTON):
        diagonal = porosity * sat_slope(current)
        current_ext = padded(current, (("gx", 1), ("gy", 2)), 1)
        faces = coefficients(current_ext, cond_ext, act_ext)
        remainder = -newton_residual(
            current_ext, faces, pressure_old, porosity, recharge, active_cells
        )
        first_norm = jnp.sqrt(lax.psum(jnp.sum(remainder * remainder), ("gx", "gy")) + epsilon)
        basis_one = remainder / first_norm
        basis_ext = padded(basis_one, (("gx", 1), ("gy", 2)), 1)
        image_one = jacobian_apply(basis_ext, faces, diagonal, active_cells)
        entry_one, square_one = lax.psum(
            (jnp.sum(image_one * basis_one), jnp.sum(image_one * image_one)), ("gx", "gy")
        )
        ortho_one = image_one - entry_one * basis_one
        entry_two = jnp.sqrt(square_one - entry_one * entry_one + epsilon)
        basis_two = ortho_one / entry_two
        second_ext = padded(basis_two, (("gx", 1), ("gy", 2)), 1)
        image_two = jacobian_apply(second_ext, faces, diagonal, active_cells)
        entry_three, entry_four, square_two = lax.psum(
            (
                jnp.sum(image_two * basis_one),
                jnp.sum(image_two * basis_two),
                jnp.sum(image_two * image_two),
            ),
            ("gx", "gy"),
        )
        entry_five = jnp.sqrt(
            square_two - entry_three * entry_three - entry_four * entry_four + epsilon
        )
        weight_one, weight_two = least_squares(
            first_norm, entry_one, entry_two, entry_three, entry_four, entry_five
        )
        current = current + (weight_one * basis_one + weight_two * basis_two)
        leftover = remainder - weight_one * image_one - weight_two * image_two
    return (current, leftover)


def solution(mesh):
    placed = (
        P(None, "gx", "gy"),
        P(None, "gx", "gy"),
        P(None, "gx", "gy"),
        P(None, "gx", "gy"),
        P("gx", "gy"),
        P("gx", "gy"),
    )
    return jax.shard_map(
        body,
        mesh=mesh,
        in_specs=placed,
        out_specs=(P(None, "gx", "gy"), P(None, "gx", "gy")),
        check_vma=False,
    )
```

profile of v0, /device:TPU:0, one launch (start us, length us, event | category | flops | bytes accessed | tf_op | source)
XLA Modules:
  0.0 456.5 jit_solution(16044023497651873286)
XLA Ops:
  2.7 4.9 %collective-permute-start = (f32[11,1,512]{2,1,0:T(1,128)S(1)}, f32[11,1,512]{2,1,0:T(1,128)S(1)}, u32[]{:S(2)}, u32[]{:S(2)}) collective-permute-start(f32[11,1,512]{2,1,0:T(1,128)S(1)} %get-tuple-element.44), channel_id=1, source_target_pairs={{0,4},{4,8},{8,12},{12,16},{16,20},{20,24},{24,28},{1,5},{5,9},{9,... | collective-permute-start | bytes 67592 | tf_op jit(solution)/shard_map/ppermute | solution.py:22
  7.6 1.3 collective-permute-start.1
  9.0 1.3 collective-permute-start.5
  10.3 5.2 %collective-permute-start.4 = (f32[10,1,512]{2,1,0:T(1,128)S(1)}, f32[10,1,512]{2,1,0:T(1,128)S(1)}, u32[]{:S(2)}, u32[]{:S(2)}) collective-permute-start(f32[10,1,512]{2,1,0:T(1,128)S(1)} %get-tuple-element.68), channel_id=1, source_target_pairs={{0,4},{4,8},{8,12},{12,16},{16,20},{20,24},{24,28},{1,5},{5,9},{9,... | collective-permute-start | bytes 61448 | tf_op jit(solution)/shard_map/ppermute | solution.py:22
  18.3 1.3 collective-permute-start.2
  19.6 1.3 collective-permute-start.3
  22.0 5.5 %collective-permute-start.6 = (f32[10,66,1]{2,1,0:T(8,128)}, f32[10,66,1]{2,1,0:T(8,128)}, u32[]{:S(2)}, u32[]{:S(2)}) collective-permute-start(f32[10,66,1]{2,1,0:T(8,128)} %get-tuple-element.56), channel_id=1, source_target_pairs={{0,1},{1,2},{2,3},{4,5},{5,6},{6,7},{8,9},{9,10},{10,11},{12,13},{... | collective-permute-start | bytes 7928 | tf_op jit(solution)/shard_map/ppermute | solution.py:22
  27.5 1.3 collective-permute-start.7
  28.8 1.7 dynamic-update-slice.1
  32.4 1.7 multiply_multiply_fusion.7
  35.3 4.8 %multiply_multiply_fusion.1 = (f32[10,64,513]{2,1,0:T(8,128)S(1)}, f32[10,64,513]{2,1,0:T(8,128)}) fusion(f32[10,66,1]{2,1,0:T(8,128)} %collective-permute-done.7, f32[10,1,512]{2,1,0:T(1,128)S(1)} %collective-permute-done.5, f32[10,64,512]{2,1,0:T(8,128)S(1)} %copy-done, f32[10,1,512]{2,1,0:T(1,128)S(1)} %collective-permute-done.4, ...), kind=kLoop, calls=%fused_computation.69 | loop fusion | flops 9849600 | bytes 5738832 | tf_op jit(solution)/shard_map/mul | solution.py:52
  40.1 2.9 multiply_reduce_fusion.11
  43.0 43.8 %psum.84 = f32[]{:T(128)} all-reduce(f32[]{:T(128)} %get-tuple-element.36), channel_id=1, replica_groups=mesh['gx'=8,'gy'=4] {'gx','gy'}, use_global_device_ids=true, to_apply=%region_1.0 | all-reduce | flops 1 | bytes 8 | tf_op jit(solution)/shard_map/psum | solution.py:145
  87.5 1.6 negate_divide_fusion
  89.1 4.2 collective-permute-start.8
  93.3 1.3 collective-permute-start.9
  95.4 3.5 collective-permute-done.9
  99.2 1.3 collective-permute-start.10
  100.5 1.6 collective-permute-start.11
  102.1 3.0 fusion.18
  105.2 4.7 %fusion.10 = (f32[10,64,513]{2,1,0:T(8,128)S(1)}, f32[10,64,513]{2,1,0:T(8,128)}, f32[10,64,513]{2,1,0:T(8,128)}) fusion(f32[10,66,1]{2,1,0:T(8,128)S(1)} %collective-permute-done.11, f32[10,1,512]{2,1,0:T(1,128)S(1)} %collective-permute-done.9, f32[10,64,512]{2,1,0:T(8,128)S(1)} %negate_divide_fusion, f32[10,1,512]{2,1,0:T(1,128)S(1)} %collective-permute-done.8, ...), kind=kLoop, calls=%fused_computation.37 | loop fusion | flops 11819520 | bytes 7967040 | tf_op jit(solution)/shard_map/add | solution.py:103
  110.0 3.0 multiply_reduce_fusion.10
  112.9 45.4 %all-reduce.16 = (f32[]{:T(128)}, f32[]{:T(128)}) all-reduce(f32[]{:T(128)} %get-tuple-element.11, f32[]{:T(128)} %get-tuple-element.10), channel_id=1, replica_groups=mesh['gx'=8,'gy'=4] {'gx','gy'}, use_global_device_ids=true, to_apply=%region_5.0 | all-reduce | flops 2 | bytes 16 | tf_op jit(solution)/shard_map/psum | solution.py:149
  160.3 2.8 subtract_divide_fusion.1
  163.1 4.2 collective-permute-start.12
  167.3 1.3 collective-permute-start.13
  168.6 1.8 fusion.56
  171.2 1.8 collective-permute-done.13
  173.2 1.3 collective-permute-start.14
  174.5 1.3 collective-permute-start.15
  175.8 2.1 fusion.19
  180.6 2.0 multiply_reduce_fusion.6
  182.6 46.0 %all-reduce.15 = (f32[]{:T(128)}, f32[]{:T(128)}, f32[]{:T(128)}) all-reduce(f32[]{:T(128)} %get-tuple-element.8, f32[]{:T(128)} %get-tuple-element.9, f32[]{:T(128)} %get-tuple-element.7), channel_id=1, replica_groups=mesh['gx'=8,'gy'=4] {'gx','gy'}, use_global_device_ids=true, to_apply=%region_9.0 | all-reduce | flops 3 | bytes 24 | tf_op jit(solution)/shard_map/psum | solution.py:157
  234.3 2.3 add_add_fusion.1
  236.7 4.2 collective-permute-start.16
  240.9 1.3 collective-permute-start.17
  242.7 3.9 collective-permute-done.17
  246.7 1.3 collective-permute-start.18
  248.1 1.6 collective-permute-start.19
  251.0 1.2 collective-permute-done.19
  254.2 3.0 multiply_reduce_fusion.5
  257.2 45.9 %psum.90 = f32[]{:T(128)} all-reduce(f32[]{:T(128)} %get-tuple-element.27), channel_id=1, replica_groups=mesh['gx'=8,'gy'=4] {'gx','gy'}, use_global_device_ids=true, to_apply=%region_13.0 | all-reduce | flops 1 | bytes 8 | tf_op jit(solution)/shard_map/psum | solution.py:145
  303.7 1.6 negate_divide_fusion.1
  305.4 4.2 collective-permute-start.20
  309.5 1.3 collective-permute-start.21
  311.7 3.5 collective-permute-done.21
  315.4 1.3 collective-permute-start.22
  316.8 1.4 collective-permute-start.23
  318.2 1.8 fusion.20
  320.9 3.5 fusion.4
  324.4 2.9 multiply_reduce_fusion.4
  327.4 46.0 %all-reduce.14 = (f32[]{:T(128)}, f32[]{:T(128)}) all-reduce(f32[]{:T(128)} %get-tuple-element.6, f32[]{:T(128)} %get-tuple-element.5), channel_id=1, replica_groups=mesh['gx'=8,'gy'=4] {'gx','gy'}, use_global_device_ids=true, to_apply=%region_17.0 | all-reduce | flops 2 | bytes 16 | tf_op jit(solution)/shard_map/psum | solution.py:149
  375.4 2.7 subtract_divide_fusion
  378.2 4.2 collective-permute-start.24
  382.4 1.3 collective-permute-start.25
  383.7 1.9 fusion.54
  386.3 1.7 collective-permute-done.25
  388.1 1.3 pad_maximum_fusion.57
  389.3 1.3 collective-permute-start.26
  390.7 1.8 collective-permute-start.27
  392.5 1.8 fusion.21
  397.1 3.0 multiply_reduce_fusion
  400.1 46.0 %all-reduce.13 = (f32[]{:T(128)}, f32[]{:T(128)}, f32[]{:T(128)}) all-reduce(f32[]{:T(128)} %get-tuple-element.3, f32[]{:T(128)} %get-tuple-element.4, f32[]{:T(128)} %get-tuple-element.2), channel_id=1, replica_groups=mesh['gx'=8,'gy'=4] {'gx','gy'}, use_global_device_ids=true, to_apply=%region_21.0 | all-reduce | flops 3 | bytes 24 | tf_op jit(solution)/shard_map/psum | solution.py:157
  452.1 4.4 multiply_subtract_fusion
  (140 shorter events, 21.7 us)
Async XLA Ops:
  0.6 14.8 %copy-start.44 = (s32[64,512]{1,0:T(8,128)S(1)}, s32[64,512]{1,0:T(8,128)}, u32[]{:S(2)}) copy-start(s32[64,512]{1,0:T(8,128)} %param.11) | copy-start | bytes 393220
  0.6 8.3 %copy-start = (f32[10,64,512]{2,1,0:T(8,128)S(1)}, f32[10,64,512]{2,1,0:T(8,128)}, u32[]{:S(2)}) copy-start(f32[10,64,512]{2,1,0:T(8,128)} %param.6) | copy-start | bytes 3932164
  2.7 13.9 %collective-permute-start = (f32[11,1,512]{2,1,0:T(1,128)S(1)}, f32[11,1,512]{2,1,0:T(1,128)S(1)}, u32[]{:S(2)}, u32[]{:S(2)}) collective-permute-start(f32[11,1,512]{2,1,0:T(1,128)S(1)} %get-tuple-element.44), channel_id=1, source_target_pairs={{0,4},{4,8},{8,12},{12,16},{16,20},{20,24},{24,28},{1,5},{5,9},{9,... | collective-permute-start | bytes 67592 | tf_op jit(solution)/shard_map/ppermute | solution.py:22
  7.6 9.0 %collective-permute-start.1 = (f32[11,1,512]{2,1,0:T(1,128)S(1)}, f32[11,1,512]{2,1,0:T(1,128)S(1)}, u32[]{:S(2)}, u32[]{:S(2)}) collective-permute-start(f32[11,1,512]{2,1,0:T(1,128)S(1)} %get-tuple-element.45), channel_id=1, source_target_pairs={{4,0},{8,4},{12,8},{16,12},{20,16},{24,20},{28,24},{5,1},{9,5},{13... | collective-permute-start | bytes 67592 | tf_op jit(solution)/shard_map/ppermute | solution.py:24
  9.0 12.0 %collective-permute-start.5 = (f32[10,1,512]{2,1,0:T(1,128)S(1)}, f32[10,1,512]{2,1,0:T(1,128)S(1)}, u32[]{:S(2)}, u32[]{:S(2)}) collective-permute-start(f32[10,1,512]{2,1,0:T(1,128)S(1)} %get-tuple-element.69), channel_id=1, source_target_pairs={{4,0},{8,4},{12,8},{16,12},{20,16},{24,20},{28,24},{5,1},{9,5},{13... | collective-permute-start | bytes 61448 | tf_op jit(solution)/shard_map/ppermute | solution.py:24
  10.3 10.7 %collective-permute-start.4 = (f32[10,1,512]{2,1,0:T(1,128)S(1)}, f32[10,1,512]{2,1,0:T(1,128)S(1)}, u32[]{:S(2)}, u32[]{:S(2)}) collective-permute-start(f32[10,1,512]{2,1,0:T(1,128)S(1)} %get-tuple-element.68), channel_id=1, source_target_pairs={{0,4},{4,8},{8,12},{12,16},{16,20},{20,24},{24,28},{1,5},{5,9},{9,... | collective-permute-start | bytes 61448 | tf_op jit(solution)/shard_map/ppermute | solution.py:22
  15.5 1.8 copy-start.1
  18.3 12.1 %collective-permute-start.2 = (f32[11,66,1]{2,1,0:T(8,128)}, f32[11,66,1]{2,1,0:T(8,128)S(1)}, u32[]{:S(2)}, u32[]{:S(2)}) collective-permute-start(f32[11,66,1]{2,1,0:T(8,128)} %get-tuple-element.42), channel_id=1, source_target_pairs={{0,1},{1,2},{2,3},{4,5},{5,6},{6,7},{8,9},{9,10},{10,11},{12,13},{... | collective-permute-start | bytes 8720 | tf_op jit(solution)/shard_map/ppermute | solution.py:22
  19.6 10.8 %collective-permute-start.3 = (f32[11,66,1]{2,1,0:T(8,128)}, f32[11,66,1]{2,1,0:T(8,128)}, u32[]{:S(2)}, u32[]{:S(2)}) collective-permute-start(f32[11,66,1]{2,1,0:T(8,128)} %get-tuple-element.43), channel_id=1, source_target_pairs={{1,0},{2,1},{3,2},{5,4},{6,5},{7,6},{9,8},{10,9},{11,10},{13,12},{... | collective-permute-start | bytes 8720 | tf_op jit(solution)/shard_map/ppermute | solution.py:24
  22.0 13.2 %collective-permute-start.6 = (f32[10,66,1]{2,1,0:T(8,128)}, f32[10,66,1]{2,1,0:T(8,128)}, u32[]{:S(2)}, u32[]{:S(2)}) collective-permute-start(f32[10,66,1]{2,1,0:T(8,128)} %get-tuple-element.56), channel_id=1, source_target_pairs={{0,1},{1,2},{2,3},{4,5},{5,6},{6,7},{8,9},{9,10},{10,11},{12,13},{... | collective-permute-start | bytes 7928 | tf_op jit(solution)/shard_map/ppermute | solution.py:22
  27.5 7.8 %collective-permute-start.7 = (f32[10,66,1]{2,1,0:T(8,128)}, f32[10,66,1]{2,1,0:T(8,128)}, u32[]{:S(2)}, u32[]{:S(2)}) collective-permute-start(f32[10,66,1]{2,1,0:T(8,128)} %get-tuple-element.57), channel_id=1, source_target_pairs={{1,0},{2,1},{3,2},{5,4},{6,5},{7,6},{9,8},{10,9},{11,10},{13,12},{... | collective-permute-start | bytes 7928 | tf_op jit(solution)/shard_map/ppermute | solution.py:24
  35.3 4.8 %copy-start.7 = (f32[10,64,512]{2,1,0:T(8,128)S(1)}, f32[10,64,512]{2,1,0:T(8,128)}, u32[]{:S(2)}) copy-start(f32[10,64,512]{2,1,0:T(8,128)} %param.9) | copy-start | bytes 3932164
  35.3 4.8 %copy-start.32 = (f32[10,64,512]{2,1,0:T(8,128)S(1)}, f32[10,64,512]{2,1,0:T(8,128)}, u32[]{:S(2)}) copy-start(f32[10,64,512]{2,1,0:T(8,128)} %param.7) | copy-start | bytes 3932164
  35.3 4.8 %copy-start.42 = (f32[64,512]{1,0:T(8,128)S(1)}, f32[64,512]{1,0:T(8,128)}, u32[]{:S(2)}) copy-start(f32[64,512]{1,0:T(8,128)} %param.10) | copy-start | bytes 393220
  87.5 7.1 %copy-start.17 = (f32[9,64,512]{2,1,0:T(8,128)S(1)}, f32[9,64,512]{2,1,0:T(8,128)}, u32[]{:S(2)}) copy-start(f32[9,64,512]{2,1,0:T(8,128)} %get-tuple-element.39) | copy-start | bytes 3538948
  89.1 6.3 %collective-permute-start.8 = (f32[10,1,512]{2,1,0:T(1,128)S(1)}, f32[10,1,512]{2,1,0:T(1,128)S(1)}, u32[]{:S(2)}, u32[]{:S(2)}) collective-permute-start(f32[10,1,512]{2,1,0:T(1,128)S(1)} %get-tuple-element.66), channel_id=1, source_target_pairs={{0,4},{4,8},{8,12},{12,16},{16,20},{20,24},{24,28},{1,5},{5,9},{9,... | collective-permute-start | bytes 61448 | tf_op jit(solution)/shard_map/ppermute | solution.py:22
  93.3 5.7 %collective-permute-start.9 = (f32[10,1,512]{2,1,0:T(1,128)S(1)}, f32[10,1,512]{2,1,0:T(1,128)S(1)}, u32[]{:S(2)}, u32[]{:S(2)}) collective-permute-start(f32[10,1,512]{2,1,0:T(1,128)S(1)} %get-tuple-element.67), channel_id=1, source_target_pairs={{4,0},{8,4},{12,8},{16,12},{20,16},{24,20},{28,24},{5,1},{9,5},{13... | collective-permute-start | bytes 61448 | tf_op jit(solution)/shard_map/ppermute | solution.py:24
  95.4 6.7 %copy-start.26 = (f32[10,65,512]{2,1,0:T(8,128)S(1)}, f32[10,65,512]{2,1,0:T(8,128)}, u32[]{:S(2)}) copy-start(f32[10,65,512]{2,1,0:T(8,128)} %dynamic-update-slice.1) | copy-start | bytes 3993604
  99.2 6.0 %collective-permute-start.10 = (f32[10,66,1]{2,1,0:T(8,128)S(1)}, f32[10,66,1]{2,1,0:T(8,128)S(1)}, u32[]{:S(2)}, u32[]{:S(2)}) collective-permute-start(f32[10,66,1]{2,1,0:T(8,128)S(1)} %get-tuple-element.54), channel_id=1, source_target_pairs={{0,1},{1,2},{2,3},{4,5},{5,6},{6,7},{8,9},{9,10},{10,11},{12,13},{... | collective-permute-start | bytes 7928 | tf_op jit(solution)/shard_map/ppermute | solution.py:22
  100.5 4.8 %copy-start.22 = (f32[10,64,513]{2,1,0:T(8,128)S(1)}, f32[10,64,513]{2,1,0:T(8,128)}, u32[]{:S(2)}) copy-start(f32[10,64,513]{2,1,0:T(8,128)} %get-tuple-element.41) | copy-start | bytes 3939844
  100.5 4.7 %collective-permute-start.11 = (f32[10,66,1]{2,1,0:T(8,128)S(1)}, f32[10,66,1]{2,1,0:T(8,128)S(1)}, u32[]{:S(2)}, u32[]{:S(2)}) collective-permute-start(f32[10,66,1]{2,1,0:T(8,128)S(1)} %get-tuple-element.55), channel_id=1, source_target_pairs={{1,0},{2,1},{3,2},{5,4},{6,5},{7,6},{9,8},{10,9},{11,10},{13,12},{... | collective-permute-start | bytes 7928 | tf_op jit(solution)/shard_map/ppermute | solution.py:24
  105.2 4.7 %copy-start.8 = (f32[10,64,512]{2,1,0:T(8,128)S(1)}, f32[10,64,512]{2,1,0:T(8,128)}, u32[]{:S(2)}) copy-start(f32[10,64,512]{2,1,0:T(8,128)} %param.9) | copy-start | bytes 3932164
  105.2 4.7 %copy-start.13 = (f32[10,64,512]{2,1,0:T(8,128)S(1)}, f32[10,64,512]{2,1,0:T(8,128)}, u32[]{:S(2)}) copy-start(f32[10,64,512]{2,1,0:T(8,128)} %get-tuple-element.37) | copy-start | bytes 3932164
  160.3 8.4 %copy-start.18 = (f32[9,64,512]{2,1,0:T(8,128)S(1)}, f32[9,64,512]{2,1,0:T(8,128)}, u32[]{:S(2)}) copy-start(f32[9,64,512]{2,1,0:T(8,128)} %get-tuple-element.39) | copy-start | bytes 3538948
  163.1 16.2 %copy-start.3 = (f32[10,64,512]{2,1,0:T(8,128)}, f32[10,64,512]{2,1,0:T(8,128)S(1)}, u32[]{:S(2)}) copy-start(f32[10,64,512]{2,1,0:T(8,128)S(1)} %subtract_divide_fusion.1) | copy-start | bytes 3932164
  163.1 8.1 %collective-permute-start.12 = (f32[10,1,512]{2,1,0:T(1,128)S(1)}, f32[10,1,512]{2,1,0:T(1,128)S(1)}, u32[]{:S(2)}, u32[]{:S(2)}) collective-permute-start(f32[10,1,512]{2,1,0:T(1,128)S(1)} %get-tuple-element.64), channel_id=1, source_target_pairs={{0,4},{4,8},{8,12},{12,16},{16,20},{20,24},{24,28},{1,5},{5,9},{9,... | collective-permute-start | bytes 61448 | tf_op jit(solution)/shard_map/ppermute | solution.py:22
  167.3 5.7 %collective-permute-start.13 = (f32[10,1,512]{2,1,0:T(1,128)S(1)}, f32[10,1,512]{2,1,0:T(1,128)S(1)}, u32[]{:S(2)}, u32[]{:S(2)}) collective-permute-start(f32[10,1,512]{2,1,0:T(1,128)S(1)} %get-tuple-element.65), channel_id=1, source_target_pairs={{4,0},{8,4},{12,8},{16,12},{20,16},{24,20},{28,24},{5,1},{9,5},{13... | collective-permute-start | bytes 61448 | tf_op jit(solution)/shard_map/ppermute | solution.py:24
  171.2 4.6 %copy-start.31 = (f32[10,65,512]{2,1,0:T(8,128)S(1)}, f32[10,65,512]{2,1,0:T(8,128)}, u32[]{:S(2)}) copy-start(f32[10,65,512]{2,1,0:T(8,128)} %get-tuple-element.31) | copy-start | bytes 3993604
  173.2 4.7 %collective-permute-start.14 = (f32[10,66,1]{2,1,0:T(8,128)S(1)}, f32[10,66,1]{2,1,0:T(8,128)S(1)}, u32[]{:S(2)}, u32[]{:S(2)}) collective-permute-start(f32[10,66,1]{2,1,0:T(8,128)S(1)} %get-tuple-element.52), channel_id=1, source_target_pairs={{0,1},{1,2},{2,3},{4,5},{5,6},{6,7},{8,9},{9,10},{10,11},{12,13},{... | collective-permute-start | bytes 7928 | tf_op jit(solution)/shard_map/ppermute | solution.py:22
  174.5 4.0 collective-permute-start.15
  175.8 2.7 copy-start.29
  175.8 2.7 copy-start.30
  178.6 2.1 copy-start.34
  234.3 7.9 %copy-start.19 = (f32[9,64,512]{2,1,0:T(8,128)S(1)}, f32[9,64,512]{2,1,0:T(8,128)}, u32[]{:S(2)}) copy-start(f32[9,64,512]{2,1,0:T(8,128)} %get-tuple-element.39) | copy-start | bytes 3538948
  236.7 6.0 %collective-permute-start.16 = (f32[10,1,512]{2,1,0:T(1,128)S(1)}, f32[10,1,512]{2,1,0:T(1,128)S(1)}, u32[]{:S(2)}, u32[]{:S(2)}) collective-permute-start(f32[10,1,512]{2,1,0:T(1,128)S(1)} %get-tuple-element.62), channel_id=1, source_target_pairs={{0,4},{4,8},{8,12},{12,16},{16,20},{20,24},{24,28},{1,5},{5,9},{9,... | collective-permute-start | bytes 61448 | tf_op jit(solution)/shard_map/ppermute | solution.py:22
  240.9 5.7 %collective-permute-start.17 = (f32[10,1,512]{2,1,0:T(1,128)S(1)}, f32[10,1,512]{2,1,0:T(1,128)S(1)}, u32[]{:S(2)}, u32[]{:S(2)}) collective-permute-start(f32[10,1,512]{2,1,0:T(1,128)S(1)} %get-tuple-element.63), channel_id=1, source_target_pairs={{4,0},{8,4},{12,8},{16,12},{20,16},{24,20},{28,24},{5,1},{9,5},{13... | collective-permute-start | bytes 61448 | tf_op jit(solution)/shard_map/ppermute | solution.py:24
  242.7 7.1 %copy-start.2 = (f32[10,64,512]{2,1,0:T(8,128)S(1)}, f32[10,64,512]{2,1,0:T(8,128)}, u32[]{:S(2)}) copy-start(f32[10,64,512]{2,1,0:T(8,128)} %param.8) | copy-start | bytes 3932164
  246.7 4.2 collective-permute-start.18
  248.1 4.9 %copy-start.23 = (f32[10,64,513]{2,1,0:T(8,128)S(1)}, f32[10,64,513]{2,1,0:T(8,128)}, u32[]{:S(2)}) copy-start(f32[10,64,513]{2,1,0:T(8,128)} %get-tuple-element.41) | copy-start | bytes 3939844
  248.1 4.2 collective-permute-start.19
  250.9 3.3 copy-start.10
  251.0 3.2 copy-start.33
  251.0 3.2 copy-start.43
  303.7 7.1 %copy-start.20 = (f32[9,64,512]{2,1,0:T(8,128)S(1)}, f32[9,64,512]{2,1,0:T(8,128)}, u32[]{:S(2)}) copy-start(f32[9,64,512]{2,1,0:T(8,128)} %get-tuple-element.39) | copy-start | bytes 3538948
  305.4 6.3 %collective-permute-start.20 = (f32[10,1,512]{2,1,0:T(1,128)S(1)}, f32[10,1,512]{2,1,0:T(1,128)S(1)}, u32[]{:S(2)}, u32[]{:S(2)}) collective-permute-start(f32[10,1,512]{2,1,0:T(1,128)S(1)} %get-tuple-element.60), channel_id=1, source_target_pairs={{0,4},{4,8},{8,12},{12,16},{16,20},{20,24},{24,28},{1,5},{5,9},{9,... | collective-permute-start | bytes 61448 | tf_op jit(solution)/shard_map/ppermute | solution.py:22
  309.5 5.7 %collective-permute-start.21 = (f32[10,1,512]{2,1,0:T(1,128)S(1)}, f32[10,1,512]{2,1,0:T(1,128)S(1)}, u32[]{:S(2)}, u32[]{:S(2)}) collective-permute-start(f32[10,1,512]{2,1,0:T(1,128)S(1)} %get-tuple-element.61), channel_id=1, source_target_pairs={{4,0},{8,4},{12,8},{16,12},{20,16},{24,20},{28,24},{5,1},{9,5},{13... | collective-permute-start | bytes 61448 | tf_op jit(solution)/shard_map/ppermute | solution.py:24
  315.4 4.6 %collective-permute-start.22 = (f32[10,66,1]{2,1,0:T(8,128)S(1)}, f32[10,66,1]{2,1,0:T(8,128)S(1)}, u32[]{:S(2)}, u32[]{:S(2)}) collective-permute-start(f32[10,66,1]{2,1,0:T(8,128)S(1)} %get-tuple-element.48), channel_id=1, source_target_pairs={{0,1},{1,2},{2,3},{4,5},{5,6},{6,7},{8,9},{9,10},{10,11},{12,13},{... | collective-permute-start | bytes 7928 | tf_op jit(solution)/shard_map/ppermute | solution.py:22
  316.7 4.2 copy-start.24
  316.7 4.2 copy-start.39
  316.8 4.2 copy-start.41
  316.8 4.1 collective-permute-start.23
  320.0 4.4 copy-start.11
  320.1 4.4 copy-start.15
  375.4 8.3 %copy-start.21 = (f32[9,64,512]{2,1,0:T(8,128)S(1)}, f32[9,64,512]{2,1,0:T(8,128)}, u32[]{:S(2)}) copy-start(f32[9,64,512]{2,1,0:T(8,128)} %get-tuple-element.39) | copy-start | bytes 3538948
  378.1 5.5 %copy-start.4 = (f32[10,64,512]{2,1,0:T(8,128)}, f32[10,64,512]{2,1,0:T(8,128)S(1)}, u32[]{:S(2)}) copy-start(f32[10,64,512]{2,1,0:T(8,128)S(1)} %subtract_divide_fusion) | copy-start | bytes 3932164
  378.2 8.1 %collective-permute-start.24 = (f32[10,1,512]{2,1,0:T(1,128)S(1)}, f32[10,1,512]{2,1,0:T(1,128)S(1)}, u32[]{:S(2)}, u32[]{:S(2)}) collective-permute-start(f32[10,1,512]{2,1,0:T(1,128)S(1)} %get-tuple-element.58), channel_id=1, source_target_pairs={{0,4},{4,8},{8,12},{12,16},{16,20},{20,24},{24,28},{1,5},{5,9},{9,... | collective-permute-start | bytes 61448 | tf_op jit(solution)/shard_map/ppermute | solution.py:22
  382.4 5.7 %collective-permute-start.25 = (f32[10,1,512]{2,1,0:T(1,128)S(1)}, f32[10,1,512]{2,1,0:T(1,128)S(1)}, u32[]{:S(2)}, u32[]{:S(2)}) collective-permute-start(f32[10,1,512]{2,1,0:T(1,128)S(1)} %get-tuple-element.59), channel_id=1, source_target_pairs={{4,0},{8,4},{12,8},{16,12},{20,16},{24,20},{28,24},{5,1},{9,5},{13... | collective-permute-start | bytes 61448 | tf_op jit(solution)/shard_map/ppermute | solution.py:24
  386.3 6.2 %copy-start.5 = (f32[10,64,512]{2,1,0:T(8,128)S(1)}, f32[10,64,512]{2,1,0:T(8,128)}, u32[]{:S(2)}) copy-start(f32[10,64,512]{2,1,0:T(8,128)} %copy-done.4) | copy-start | bytes 3932164
  389.3 5.0 %collective-permute-start.26 = (f32[10,66,1]{2,1,0:T(8,128)S(1)}, f32[10,66,1]{2,1,0:T(8,128)S(1)}, u32[]{:S(2)}, u32[]{:S(2)}) collective-permute-start(f32[10,66,1]{2,1,0:T(8,128)S(1)} %get-tuple-element.46), channel_id=1, source_target_pairs={{0,1},{1,2},{2,3},{4,5},{5,6},{6,7},{8,9},{9,10},{10,11},{12,13},{... | collective-permute-start | bytes 7928 | tf_op jit(solution)/shard_map/ppermute | solution.py:22
  390.7 4.4 copy-start.27
  390.7 4.4 copy-start.28
  390.7 4.3 collective-permute-start.27
  395.0 2.1 copy-start.35
  397.1 55.0 %copy-start.6 = (f32[10,64,512]{2,1,0:T(8,128)S(1)}, f32[10,64,512]{2,1,0:T(8,128)}, u32[]{:S(2)}) copy-start(f32[10,64,512]{2,1,0:T(8,128)} %copy-done.4) | copy-start | bytes 3932164
  (9 other events, 11.7 us)
where the time goes:
time: 459 us; the launch traced here: 457 us
  blocking collectives  273 us (59%)
  other arithmetic  73.5 us (16%)
  starting transfers between devices  63.7 us (14%)
  between operations  20 us (4%)
  waiting for transfers between devices  18 us (4%)
  local copies, waits for them, and re-layouts  8.12 us (2%)
    psum x2, blocking collectives, body(): lax.psum((jnp.sum(image_two * basis_one), jnp.sum(image_two * basis_two),...  92.1 us
    psum x2, blocking collectives, body(): lax.psum((jnp.sum(image_one * basis_one), jnp.sum(image_one * image_one))...  91.4 us
    psum x2, blocking collectives, body(): lax.psum(jnp.sum(remainder * remainder), ('gx', 'gy')) + epsilon  89.7 us
    ppermute x14, starting transfers between devices, padded(): lax.ppermute(tail, axis, [(i, (i + 1) % count) for i in range(ends)])  44.3 us
    ppermute x14, starting transfers between devices, padded(): lax.ppermute(head, axis, [((i + 1) % count, i) for i in range(ends)])  19.4 us
    ppermute x14, waiting for transfers between devices, padded(): lax.ppermute(head, axis, [((i + 1) % count, i) for i in range(ends)])  18 us
    mul x6, other arithmetic, face_pair(): return (coef_low, coef_high, transmit * mobility * head_drop)  10.4 us
    add x4, other arithmetic, jacobian_apply(): flow_y = y_low * vector[:, 1:-1, :-1] + y_high * vector[:, 1:-1, 1:]  9.56 us
  transfers between devices with their start and end apart: 28, of which 10 were waited for; matrix products, arithmetic and copies ran while one was open for 5% of the time, Pallas kernels for 0%

commit v1 on v0

v1 whole, which is shorter than its diff:
```python
import functools

import jax
import jax.numpy as jnp
from jax import lax
from jax.experimental import pallas as pl
from jax.experimental.pallas import tpu as pltpu
from jax.sharding import PartitionSpec as P

NEWTON = 2
residual_sat = 0.1
vertical_factor = 2.0
epsilon = 1e-06
T = 8
W = 128
MESH = pl.DeviceIdType.MESH


def sigmoid(v):
    return 1.0 / (1.0 + jnp.exp(jnp.minimum(-v, 87.0)))


def fold(v):
    out = v[:, :W]
    for j in range(1, v.shape[1] // W):
        out = out + v[:, j * W:(j + 1) * W]
    return out


def kernel(
    L, NX, NY, GX, GY,
    p_in, po_in, k_in, por_in, rech_in, act_in,
    p_out, l_out,
    pre, sre, are, bre, cre, acte, p9, r0,
    txp, txm, typ, tym, tzp,
    dg, oxp, oxm, oyp, oym, ozp, ozm,
    srow, scol, rrow, rcol, sumy, sumx,
    send_sem, recv_sem, ysend, yrecv, xsend, xrecv,
):
    R = NX // T
    gx = lax.axis_index("gx")
    gy = lax.axis_index("gy")
    f32 = jnp.float32
    row8 = lax.broadcasted_iota(jnp.int32, (T, NY), 0)
    lane = lax.broadcasted_iota(jnp.int32, (T, NY), 1)
    lane1 = lax.broadcasted_iota(jnp.int32, (T, W), 1)
    has = (gx > 0, gx < GX - 1, gy > 0, gy < GY - 1)

    rrow[...] = jnp.zeros_like(rrow)
    rcol[...] = jnp.zeros_like(rcol)

    barrier = pltpu.get_barrier_semaphore()
    for d in range(1, GX):
        pl.semaphore_signal(barrier, inc=1, device_id=(lax.rem(gx + d, GX), gy), device_id_type=MESH)
    for d in range(1, GY):
        pl.semaphore_signal(barrier, inc=1, device_id=(gx, lax.rem(gy + d, GY)), device_id_type=MESH)

    def tile(ref, k, r):
        return ref[k, pl.ds(pl.multiple_of((r + 1) * T, T), T), :]

    def plain(ref, k, r):
        return ref[k, pl.ds(pl.multiple_of(r * T, T), T), :]

    def put(ref, k, r, v):
        ref[k, pl.ds(pl.multiple_of(r * T, T), T), :] = v

    def up(ref, k, r, cur):
        return pltpu.roll(jnp.where(row8 == T - 1, tile(ref, k, r - 1), cur), 1, 0)

    def down(ref, k, r, cur):
        return pltpu.roll(jnp.where(row8 == 0, tile(ref, k, r + 1), cur), T - 1, 0)

    def wide(v):
        return jnp.concatenate([v] * (NY // W), axis=1)

    def left(cur, halo, k, r):
        h = pltpu.roll(halo, lax.rem(2 * W - (k * R + r), W), 1)
        return jnp.where(lane == 0, wide(h), pltpu.roll(cur, 1, 1))

    def right(cur, halo, k, r):
        h = pltpu.roll(halo, W - 1 - (k * R + r), 1)
        return jnp.where(lane == NY - 1, wide(h), pltpu.roll(cur, NY - 1, 1))

    def pack(acc, v, k, r):
        lo, hi = acc
        at = lane1 == k * R + r
        lo = jnp.where(at, jnp.broadcast_to(v[:, 0:1], (T, W)), lo)
        hi = jnp.where(at, jnp.broadcast_to(v[:, NY - 1:NY], (T, W)), hi)
        return lo, hi

    zero1 = jnp.zeros((T, W), f32)

    def copies(st, nr, nc):
        peers = ((gx - 1, gy), (gx + 1, gy), (gx, gy - 1), (gx, gy + 1))
        out = []
        for d in range(4):
            back = d ^ 1
            if d < 2:
                src, dst = srow.at[st, d, pl.ds(0, nr)], rrow.at[st, back, pl.ds(0, nr)]
            else:
                src, dst = scol.at[st, d - 2, pl.ds(0, nc)], rcol.at[st, back - 2, pl.ds(0, nc)]
            out.append((has[d], pltpu.make_async_remote_copy(
                src_ref=src, dst_ref=dst,
                send_sem=send_sem.at[st, d], recv_sem=recv_sem.at[st, back],
                device_id=peers[d], device_id_type=MESH)))
        return out

    def start(st, nr, nc):
        for cond, c in copies(st, nr, nc):
            @pl.when(cond)
            def _(c=c):
                c.start()

    def finish(st, nr, nc):
        for d, (cond, c) in enumerate(copies(st, nr, nc)):
            @pl.when(cond)
            def _(c=c):
                c.wait_send()
        cs = copies(st, nr, nc)
        for d in range(4):
            @pl.when(has[d])
            def _(d=d):
                cs[d ^ 1][1].wait_recv()

    NR0 = srow.shape[2]
    NRL = ((L + T - 1) // T) * T

    for e, row in ((0, 0), (1, NX - 1)):
        for k in range(L):
            srow[0, e, k:k + 1, :] = p_in[k, row:row + 1, :]
            srow[0, e, L + k:L + k + 1, :] = k_in[k, row:row + 1, :]
        srow[0, e, 2 * L:2 * L + 1, :] = act_in[row:row + 1, :].astype(f32)

    def pack0(r, c):
        pp, kk, aa = c
        for k in range(L):
            pp = pack(pp, plain(p_in, k, r), k, r)
            kk = pack(kk, plain(k_in, k, r), k, r)
        aa = pack(aa, act_in[pl.ds(pl.multiple_of(r * T, T), T), :].astype(f32), 0, r)
        return pp, kk, aa

    z2 = (zero1, zero1)
    pp, kk, aa = lax.fori_loop(0, R, pack0, (z2, z2, z2))
    for e in range(2):
        scol[0, e, 0:T, :] = pp[e]
        scol[0, e, T:2 * T, :] = kk[e]
        scol[0, e, 2 * T:3 * T, :] = aa[e]
    pl.semaphore_wait(barrier, GX - 1 + GY - 1)
    start(0, NR0, 3 * T)

    def local(r, c):
        act = act_in[pl.ds(pl.multiple_of(r * T, T), T), :].astype(f32)
        put(acte, 0, r + 1, act)
        for k in range(L):
            p = plain(p_in, k, r)
            put(pre, k, r + 1, p)
            put(sre, k, r + 1, sigmoid(p))
            put(are, k, r + 1, plain(k_in, k, r))
            w = (1.0 - residual_sat) * act * plain(por_in, k, r)
            put(p9, k, r, w)
            base = w * sigmoid(plain(po_in, k, r))
            if k == L - 1:
                base = base + act * rech_in[pl.ds(pl.multiple_of(r * T, T), T), :]
            put(r0, k, r, base)
        return c

    lax.fori_loop(0, R, local, 0)
    finish(0, NR0, 3 * T)

    def halo_rows(ref, st, base):
        for e, row in ((0, T - 1), (1, T + NX)):
            for k in range(L):
                ref[k, row:row + 1, :] = rrow[st, e, base + k:base + k + 1, :]

    halo_rows(pre, 0, 0)
    halo_rows(are, 0, L)
    for e, row in ((0, T - 1), (1, T + NX)):
        acte[0, row:row + 1, :] = rrow[0, e, 2 * L:2 * L + 1, :]
        for k in range(L):
            sre[k, row:row + 1, :] = sigmoid(rrow[0, e, k:k + 1, :])

    kl, kh = rcol[0, 0, T:2 * T, :], rcol[0, 1, T:2 * T, :]
    al, ah = rcol[0, 0, 2 * T:3 * T, :], rcol[0, 1, 2 * T:3 * T, :]

    def trans(r, c):
        act = tile(acte, 0, r)
        ha = 0.5 * act
        a_up = ha * up(acte, 0, r, act)
        a_dn = ha * down(acte, 0, r, act)
        a_lf = ha * left(act, al, 0, r)
        a_rt = ha * right(act, ah, 0, r)
        av = vertical_factor * ha * act
        cur = tile(are, 0, r)
        for k in range(L):
            put(txm, k, r, a_up * (cur + up(are, k, r, cur)))
            put(txp, k, r, a_dn * (cur + down(are, k, r, cur)))
            put(tym, k, r, a_lf * (cur + left(cur, kl, k, r)))
            put(typ, k, r, a_rt * (cur + right(cur, kh, k, r)))
            if k < L - 1:
                nxt = tile(are, k + 1, r)
                put(tzp, k, r, av * (cur + nxt))
                cur = nxt
        return c

    lax.fori_loop(0, R, trans, 0)

    pl_c, ph_c = rcol[0, 0, 0:T, :], rcol[0, 1, 0:T, :]
    shift = jnp.zeros((1, 1), f32)
    for it in range(NEWTON):
        sl_c, sh_c = sigmoid(pl_c), sigmoid(ph_c)

        def coef(r, acc):
            act = tile(acte, 0, r)
            rest = 1.0 - act
            pc, sc = tile(pre, 0, r), tile(sre, 0, r)
            below = None
            for k in range(L):
                s2 = sc * sc
                mc = 0.5 * s2
                s1 = 1.0 - sc
                ec = s2 * s1
                sm = sd = fl = None
                for pn, sn, tr, off in (
                    (up(pre, k, r, pc), up(sre, k, r, sc), txm, oxm),
                    (down(pre, k, r, pc), down(sre, k, r, sc), txp, oxp),
                    (left(pc, pl_c, k, r), left(sc, sl_c, k, r), tym, oym),
                    (right(pc, ph_c, k, r), right(sc, sh_c, k, r), typ, oyp),
                ):
                    n2 = sn * sn
                    t = plain(tr, k, r)
                    drop = pc - pn
                    tm = t * (mc + 0.5 * n2)
                    td = t * drop
                    put(off, k, r, n2 * (1.0 - sn) * td - tm)
                    if sm is None:
                        sm, sd, fl = tm, td, tm * drop
                    else:
                        sm, sd, fl = sm + tm, sd + td, fl + tm * drop
                if below is not None:
                    tm, td, f, eb = below
                    sm, sd, fl = sm + tm, sd - td, fl - f
                    put(ozm, k, r, -(eb * td + tm))
                if k < L - 1:
                    pn, sn = tile(pre, k + 1, r), tile(sre, k + 1, r)
                    n2 = sn * sn
                    t = plain(tzp, k, r)
                    drop = pc - pn - 1.0
                    tm = t * (mc + 0.5 * n2)
                    td = t * drop
                    f = tm * drop
                    put(ozp, k, r, n2 * (1.0 - sn) * td - tm)
                    sm, sd, fl = sm + tm, sd + td, fl + f
                    below = (tm, td, f, ec)
                w = plain(p9, k, r)
                put(dg, k, r, w * sc * s1 + rest + sm + ec * sd)
                q = plain(r0, k, r) - w * sc - fl - rest * pc
                put(are, k, r + 1, q)
                acc = pack(acc, q, k, r)
                if k < L - 1:
                    pc, sc = pn, sn
            return acc

        def send(ref, st, acc):
            for e, row in ((0, T), (1, T + NX - 1)):
                for k in range(L):
                    srow[st, e, k:k + 1, :] = ref[k, row:row + 1, :]
                scol[st, e, 0:T, :] = acc[e]
            start(st, NRL, T)

        def apply(ref, k, r, cur, before, after, lo, hi):
            y = plain(dg, k, r) * cur
            y = y + plain(oxm, k, r) * up(ref, k, r, cur)
            y = y + plain(oxp, k, r) * down(ref, k, r, cur)
            y = y + plain(oym, k, r) * left(cur, lo, k, r)
            y = y + plain(oyp, k, r) * right(cur, hi, k, r)
            if before is not None:
                y = y + plain(ozm, k, r) * before
            if after is not None:
                y = y + plain(ozp, k, r) * after
            return y - shift * cur

        st = 1 + 2 * it
        acc = lax.fori_loop(0, R, coef, z2)
        send(are, st, acc)
        finish(st, NRL, T)
        halo_rows(are, st, 0)
        a_lo, a_hi = rcol[st, 0, 0:T, :], rcol[st, 1, 0:T, :]

        def first(r, c):
            acc, aa, ab, bb = c
            before, cur = None, tile(are, 0, r)
            for k in range(L):
                after = tile(are, k + 1, r) if k < L - 1 else None
                b = apply(are, k, r, cur, before, after, a_lo, a_hi)
                put(bre, k, r + 1, b)
                acc = pack(acc, b, k, r)
                aa = aa + fold(cur * cur)
                ab = ab + fold(cur * b)
                bb = bb + fold(b * b)
                before, cur = cur, after
            return acc, aa, ab, bb

        acc, aa, ab, bb = lax.fori_loop(0, R, first, (z2, zero1, zero1, zero1))
        send(bre, st + 1, acc)
        finish(st + 1, NRL, T)
        halo_rows(bre, st + 1, 0)
        b_lo, b_hi = rcol[st + 1, 0, 0:T, :], rcol[st + 1, 1, 0:T, :]
        last = it == NEWTON - 1

        def second(r, c):
            ac, bc, cc = c
            before, cur = None, tile(bre, 0, r)
            for k in range(L):
                after = tile(bre, k + 1, r) if k < L - 1 else None
                v = apply(bre, k, r, cur, before, after, b_lo, b_hi)
                if last:
                    put(cre, k, r, v)
                ac = ac + fold(tile(are, k, r) * v)
                bc = bc + fold(cur * v)
                cc = cc + fold(v * v)
                before, cur = cur, after
            return ac, bc, cc

        ac, bc, cc = lax.fori_loop(0, R, second, (zero1, zero1, zero1))

        for i, v in enumerate((aa, ab, bb, ac, bc, cc)):
            sumy[it, 0, i:i + 1, :] = jnp.sum(v, axis=0, keepdims=True)
        for i in range(6, T):
            sumy[it, 0, i:i + 1, :] = jnp.zeros((1, W), f32)

        def spread(buf, n, mine, device, ss, rs):
            cps = []
            for d in range(1, n):
                c = pltpu.make_async_remote_copy(
                    src_ref=buf.at[it, 0], dst_ref=buf.at[it, d],
                    send_sem=ss.at[it, d], recv_sem=rs.at[it, d],
                    device_id=device(lax.rem(mine + d, n)), device_id_type=MESH)
                c.start()
                cps.append(c)
            for c in cps:
                c.wait()
            tot = buf[it, 0]
            for d in range(1, n):
                tot = tot + buf[it, d]
            return tot

        tot = spread(sumy, GY, gy, lambda o: (gx, o), ysend, yrecv)
        sumx[it, 0] = tot
        tot = spread(sumx, GX, gx, lambda o: (o, gy), xsend, xrecv)
        g = jnp.sum(tot, axis=1, keepdims=True)
        aa, ab, bb, ac, bc, cc = [g[i:i + 1, :] for i in range(6)]

        n2 = aa + epsilon
        n0 = jnp.sqrt(n2)
        dl = (ab - shift * epsilon) / n2
        h11 = shift + dl
        uu = jnp.maximum(bb - 2.0 * dl * ab + dl * dl * aa, 0.0) / n2
        h21s = uu + epsilon
        h21 = jnp.sqrt(h21s)
        ze = shift - dl
        zf = -dl * shift
        za = ac + ze * ab + zf * aa
        zb = bc + ze * bb + zf * ab
        zc = cc + ze * bc + zf * ac
        sc2 = n2 * h21s
        h12 = za / (n2 * h21)
        h22 = (zb - dl * za) / sc2
        zz = (zc + ze * zb + zf * za) / sc2
        v11 = aa / n2
        v22 = uu / h21s
        v12 = h11 * epsilon / (n2 * h21)
        u2 = zz - (2.0 - v11) * h12 * h12 - (2.0 - v22) * h22 * h22 + 2.0 * h12 * h22 * v12
        h32s = jnp.maximum(u2, 0.0) + epsilon
        r1 = jnp.sqrt(h11 * h11 + h21s)
        co, si = h11 / r1, h21 / r1
        tr = co * h12 + si * h22
        lo = co * h22 - si * h12
        y2 = -lo * si * n0 / (lo * lo + h32s)
        y1 = (co * n0 - tr * y2) / r1
        w1 = y1 / n0
        w2 = y2 / (n0 * h21)
        alpha, beta = w1 - w2 * dl, w2

        if not last:
            def step(r, c):
                for k in range(L):
                    p = plain(pre, k, r) + (alpha * plain(are, k, r) + beta * plain(bre, k, r))
                    put(pre, k, r, p)
                    put(sre, k, r, sigmoid(p))
                return c

            lax.fori_loop(0, R + 2, step, 0)
            pl_c = pl_c + (alpha * a_lo + beta * b_lo)
            ph_c = ph_c + (alpha * a_hi + beta * b_hi)
            shift = h11
        else:
            ga = 1.0 - w1 * shift - w2 * zf
            gb = w1 + w2 * ze
            def end(r, c):
                for k in range(L):
                    a, b = tile(are, k, r), tile(bre, k, r)
                    put(p_out, k, r, tile(pre, k, r) + (alpha * a + beta * b))
                    put(l_out, k, r, ga * a - gb * b - w2 * plain(cre, k, r))
                return c

            lax.fori_loop(0, R, end, 0)


def body(pressure, pressure_old, conductivity, porosity, recharge, active):
    L, NX, NY = pressure.shape
    GX, GY = lax.axis_size("gx"), lax.axis_size("gy")
    f32 = jnp.float32
    cell = pltpu.VMEM((L, NX, NY), f32)
    ext = pltpu.VMEM((L, NX + 2 * T, NY), f32)
    ST = 1 + 2 * NEWTON
    NR0 = ((2 * L + 1 + T - 1) // T) * T
    dma = pltpu.SemaphoreType.DMA
    vm = pl.BlockSpec(memory_space=pltpu.VMEM)
    return pl.pallas_call(
        functools.partial(kernel, L, NX, NY, GX, GY),
        out_shape=(jax.ShapeDtypeStruct(pressure.shape, f32),) * 2,
        in_specs=[vm] * 6,
        out_specs=(vm, vm),
        scratch_shapes=[ext] * 4 + [cell, pltpu.VMEM((1, NX + 2 * T, NY), f32), cell, cell]
        + [cell] * 5 + [cell] * 7
        + [
            pltpu.VMEM((ST, 2, NR0, NY), f32), pltpu.VMEM((ST, 2, 3 * T, W), f32),
            pltpu.VMEM((ST, 2, NR0, NY), f32), pltpu.VMEM((ST, 2, 3 * T, W), f32),
            pltpu.VMEM((NEWTON, GY, T, W), f32), pltpu.VMEM((NEWTON, GX, T, W), f32),
            dma((ST, 4)), dma((ST, 4)),
            dma((NEWTON, GY)), dma((NEWTON, GY)), dma((NEWTON, GX)), dma((NEWTON, GX)),
        ],
        compiler_params=pltpu.CompilerParams(
            collective_id=0, has_side_effects=True, vmem_limit_bytes=64000000
        ),
    )(pressure, pressure_old, conductivity, porosity, recharge, active)


def solution(mesh):
    cells, flat = P(None, "gx", "gy"), P("gx", "gy")
    return jax.shard_map(
        body,
        mesh=mesh,
        in_specs=(cells, cells, cells, cells, flat, flat),
        out_specs=(cells, cells),
        check_vma=False,
    )
```

time: 459 us -> 68.1 us (0.15)
  blocking collectives: 273 us -> 0 us
  other arithmetic: 73.5 us -> 0 us
  starting transfers between devices: 63.7 us -> 0 us
  Pallas kernels: 0 us -> 63.6 us
  between operations: 20 us -> 0.65 us
  waiting for transfers between devices: 18 us -> 0 us
    psum x6 -> x0, blocking collectives: 273 us -> none  [the longest x2 92.1 us: body(): lax.psum((jnp.sum(image_two * basis_one), jnp.sum(image_two * basis_two),...]
    ppermute x28 -> x0, starting transfers between devices: 63.7 us -> none  [the longest x14 44.3 us: padded(): lax.ppermute(tail, axis, [(i, (i + 1) % count) for i in range(ends)])]
    pallas_call x0 -> x1, Pallas kernels: none -> 63.6 us  [body(): pl.pallas_call(functools.partial(kernel, L, NX, NY, GX, GY), out_shape=(j...]
    add x13 -> x0, other arithmetic: 26 us -> none  [the longest x4 9.56 us: jacobian_apply(): flow_y = y_low * vector[:, 1:-1, :-1] + y_high * vector[:, 1:-1, 1:]]
    ppermute x28 -> x0, waiting for transfers between devices: 18 us -> none  [the longest x14 18 us: padded(): lax.ppermute(head, axis, [((i + 1) % count, i) for i in range(ends)])]
    reduce_sum x6 -> x0, other arithmetic: 16.7 us -> none  [the longest x2 5.9 us: body(): jnp.sum(image_one * basis_one)]
    mul x8 -> x0, other arithmetic: 10.6 us -> none  [the longest x6 10.4 us: face_pair(): return (coef_low, coef_high, transmit * mobility * head_drop)]
    div x4 -> x0, other arithmetic: 8.69 us -> none  [the longest x2 5.56 us: body(): basis_two = ortho_one / entry_two]
  transfers between devices with their start and end apart: 28 -> 0, of which waited for: 10 -> 0; matrix products, arithmetic and copies ran while one was open for 5% -> 0% of each run, Pallas kernels for 0% -> 0%
where the time goes in v1:
time: 68.1 us; the launch traced here: 67.9 us
  Pallas kernels  63.6 us (93%)
  local copies, waits for them, and re-layouts  3.63 us (5%)
    pallas_call x1, Pallas kernels, body(): pl.pallas_call(functools.partial(kernel, L, NX, NY, GX, GY), out_shape=(j...  63.6 us
    unnamed x4, local copies, waits for them, and re-layouts  3.63 us

profile of v1, /device:TPU:0, one launch (start us, length us, event | category | flops | bytes accessed | tf_op | source)
XLA Modules:
  0.0 67.9 jit_solution(3292369373687158660)
XLA Ops:
  0.6 63.6 %shard_map.77 = (f32[10,64,512]{2,1,0:T(8,128)}, f32[10,64,512]{2,1,0:T(8,128)}) custom-call(f32[10,64,512]{2,1,0:T(8,128)} %p_in.1, f32[10,64,512]{2,1,0:T(8,128)} %po_in.1, f32[10,64,512]{2,1,0:T(8,128)} %k_in.1, f32[10,64,512]{2,1,0:T(8,128)} %por_in.1, f32[64,512]{1,0:T(8,128)} %rech_in.1, s32[64,512]{1,0:T(8,128)} %act_in.1), custom_call_target="tpu_custom_call" | custom-call | tf_op jit(solution)/shard_map/pallas_call | solution.py:419
  64.3 0.0 copy-start
  64.3 2.6 %copy.10 = f32[10,64,512]{2,1,0:T(8,128)} copy(f32[10,64,512]{2,1,0:T(8,128)} %get-tuple-element.4) | data formatting | bytes 2621440
  66.9 0.0 copy-done
  66.9 1.1 %copy.11 = f32[10,64,512]{2,1,0:T(8,128)} copy(f32[10,64,512]{2,1,0:T(8,128)S(1)} %copy-done) | data formatting | bytes 2621440
Async XLA Ops:
  64.3 2.6 %copy-start = (f32[10,64,512]{2,1,0:T(8,128)S(1)}, f32[10,64,512]{2,1,0:T(8,128)}, u32[]{:S(2)}) copy-start(f32[10,64,512]{2,1,0:T(8,128)} %get-tuple-element.5) | copy-start | bytes 3932164

commit v2 on v1

--- a/solution.py
+++ b/solution.py
@@ -29,12 +29,13 @@
 
 def kernel(
     L, NX, NY, GX, GY,
-    p_in, po_in, k_in, por_in, rech_in, act_in,
+    p_hbm, po_hbm, k_hbm, por_hbm, rech_hbm, act_hbm,
     p_out, l_out,
     pre, sre, are, bre, cre, acte, p9, r0,
     txp, txm, typ, tym, tzp,
     dg, oxp, oxm, oyp, oym, ozp, ozm,
     srow, scol, rrow, rcol, sumy, sumx,
+    act_in, rech_in, in_sem,
     send_sem, recv_sem, ysend, yrecv, xsend, xrecv,
 ):
     R = NX // T
@@ -46,6 +47,17 @@
     lane1 = lax.broadcasted_iota(jnp.int32, (T, W), 1)
     has = (gx > 0, gx < GX - 1, gy > 0, gy < GY - 1)
 
+    mid = pl.ds(T, NX)
+    loads = [
+        pltpu.make_async_copy(src, dst, in_sem.at[i])
+        for i, (src, dst) in enumerate((
+            (p_hbm, pre.at[:, mid, :]), (k_hbm, are.at[:, mid, :]), (act_hbm, act_in),
+            (rech_hbm, rech_in), (por_hbm, p9), (po_hbm, r0),
+        ))
+    ]
+    for c in loads:
+        c.start()
+
     rrow[...] = jnp.zeros_like(rrow)
     rcol[...] = jnp.zeros_like(rcol)
 
@@ -90,82 +102,86 @@
 
     zero1 = jnp.zeros((T, W), f32)
 
-    def copies(st, nr, nc):
-        peers = ((gx - 1, gy), (gx + 1, gy), (gx, gy - 1), (gx, gy + 1))
+    peers = ((gx - 1, gy), (gx + 1, gy), (gx, gy - 1), (gx, gy + 1))
+
+    def copies(st, part, n):
         out = []
-        for d in range(4):
+        for d in (0, 1) if part == 0 else (2, 3):
             back = d ^ 1
-            if d < 2:
-                src, dst = srow.at[st, d, pl.ds(0, nr)], rrow.at[st, back, pl.ds(0, nr)]
+            if part == 0:
+                src, dst = srow.at[st, d, pl.ds(0, n)], rrow.at[st, back, pl.ds(0, n)]
             else:
-                src, dst = scol.at[st, d - 2, pl.ds(0, nc)], rcol.at[st, back - 2, pl.ds(0, nc)]
-            out.append((has[d], pltpu.make_async_remote_copy(
+                src = scol.at[st, part - 1, d - 2, pl.ds(0, n)]
+                dst = rcol.at[st, part - 1, back - 2, pl.ds(0, n)]
+            out.append((has[d], has[back], pltpu.make_async_remote_copy(
                 src_ref=src, dst_ref=dst,
-                send_sem=send_sem.at[st, d], recv_sem=recv_sem.at[st, back],
+                send_sem=send_sem.at[st, part, d % 2], recv_sem=recv_sem.at[st, part, back % 2],
                 device_id=peers[d], device_id_type=MESH)))
         return out
 
-    def start(st, nr, nc):
-        for cond, c in copies(st, nr, nc):
-            @pl.when(cond)
+    def start(st, part, n):
+        for to, _, c in copies(st, part, n):
+            @pl.when(to)
             def _(c=c):
                 c.start()
 
-    def finish(st, nr, nc):
-        for d, (cond, c) in enumerate(copies(st, nr, nc)):
-            @pl.when(cond)
+    sent = []
+
+    def recv(st, part, n, also=True):
+        sent.append((st, part, n))
+        for _, frm, c in copies(st, part, n):
+            @pl.when(jnp.logical_and(frm, also))
             def _(c=c):
-                c.wait_send()
-        cs = copies(st, nr, nc)
-        for d in range(4):
-            @pl.when(has[d])
-            def _(d=d):
-                cs[d ^ 1][1].wait_recv()
+                c.wait_recv()
 
     NR0 = srow.shape[2]
     NRL = ((L + T - 1) // T) * T
 
+    for c in loads[:3]:
+        c.wait()
+
     for e, row in ((0, 0), (1, NX - 1)):
         for k in range(L):
-            srow[0, e, k:k + 1, :] = p_in[k, row:row + 1, :]
-            srow[0, e, L + k:L + k + 1, :] = k_in[k, row:row + 1, :]
+            srow[0, e, k:k + 1, :] = pre[k, T + row:T + row + 1, :]
+            srow[0, e, L + k:L + k + 1, :] = are[k, T + row:T + row + 1, :]
         srow[0, e, 2 * L:2 * L + 1, :] = act_in[row:row + 1, :].astype(f32)
 
     def pack0(r, c):
         pp, kk, aa = c
         for k in range(L):
-            pp = pack(pp, plain(p_in, k, r), k, r)
-            kk = pack(kk, plain(k_in, k, r), k, r)
+            pp = pack(pp, tile(pre, k, r), k, r)
+            kk = pack(kk, tile(are, k, r), k, r)
         aa = pack(aa, act_in[pl.ds(pl.multiple_of(r * T, T), T), :].astype(f32), 0, r)
         return pp, kk, aa
 
     z2 = (zero1, zero1)
     pp, kk, aa = lax.fori_loop(0, R, pack0, (z2, z2, z2))
     for e in range(2):
-        scol[0, e, 0:T, :] = pp[e]
-        scol[0, e, T:2 * T, :] = kk[e]
-        scol[0, e, 2 * T:3 * T, :] = aa[e]
+        scol[0, 0, e, 0:T, :] = pp[e]
+        scol[0, 0, e, T:2 * T, :] = kk[e]
+        scol[0, 0, e, 2 * T:3 * T, :] = aa[e]
     pl.semaphore_wait(barrier, GX - 1 + GY - 1)
-    start(0, NR0, 3 * T)
+    start(0, 0, NR0)
+    start(0, 1, 3 * T)
+    for c in loads[3:]:
+        c.wait()
 
     def local(r, c):
         act = act_in[pl.ds(pl.multiple_of(r * T, T), T), :].astype(f32)
         put(acte, 0, r + 1, act)
         for k in range(L):
-            p = plain(p_in, k, r)
-            put(pre, k, r + 1, p)
-            put(sre, k, r + 1, sigmoid(p))
-            put(are, k, r + 1, plain(k_in, k, r))
-            w = (1.0 - residual_sat) * act * plain(por_in, k, r)
+            put(sre, k, r + 1, sigmoid(tile(pre, k, r)))
+            w = (1.0 - residual_sat) * act * plain(p9, k, r)
             put(p9, k, r, w)
-            base = w * sigmoid(plain(po_in, k, r))
+            base = w * sigmoid(plain(r0, k, r))
             if k == L - 1:
                 base = base + act * rech_in[pl.ds(pl.multiple_of(r * T, T), T), :]
             put(r0, k, r, base)
         return c
 
     lax.fori_loop(0, R, local, 0)
-    finish(0, NR0, 3 * T)
+    recv(0, 0, NR0)
+    recv(0, 1, 3 * T)
 
     def halo_rows(ref, st, base):
         for e, row in ((0, T - 1), (1, T + NX)):
@@ -179,8 +195,8 @@
         for k in range(L):
             sre[k, row:row + 1, :] = sigmoid(rrow[0, e, k:k + 1, :])
 
-    kl, kh = rcol[0, 0, T:2 * T, :], rcol[0, 1, T:2 * T, :]
-    al, ah = rcol[0, 0, 2 * T:3 * T, :], rcol[0, 1, 2 * T:3 * T, :]
+    kl, kh = rcol[0, 0, 0, T:2 * T, :], rcol[0, 0, 1, T:2 * T, :]
+    al, ah = rcol[0, 0, 0, 2 * T:3 * T, :], rcol[0, 0, 1, 2 * T:3 * T, :]
 
     def trans(r, c):
         act = tile(acte, 0, r)
@@ -204,12 +220,42 @@
 
     lax.fori_loop(0, R, trans, 0)
 
-    pl_c, ph_c = rcol[0, 0, 0:T, :], rcol[0, 1, 0:T, :]
+    pl_c, ph_c = rcol[0, 0, 0, 0:T, :], rcol[0, 0, 1, 0:T, :]
     shift = jnp.zeros((1, 1), f32)
+    H = max(2, R - 3)
+
+    def order(i):
+        return jnp.where(i < 2, i * (R - 1), i - 1)
+
+    def emit(ref, st, i, acc):
+        @pl.when(i == 1)
+        def _():
+            for e, row in ((0, T), (1, T + NX - 1)):
+                for k in range(L):
+                    srow[st, e, k:k + 1, :] = ref[k, row:row + 1, :]
+            start(st, 0, NRL)
+
+        for part, at in ((1, H - 1), (2, R - 1)):
+            @pl.when(i == at)
+            def _(part=part):
+                scol[st, part - 1, 0, 0:T, :] = acc[0]
+                scol[st, part - 1, 1, 0:T, :] = acc[1]
+                start(st, part, T)
+
+    def ready(st, i):
+        recv(st, 2, T, i == H)
+
+    def halo(st, i):
+        late = jnp.where(i < H, 0, 1)
+        return rcol[st, late, 0, 0:T, :], rcol[st, late, 1, 0:T, :]
+
     for it in range(NEWTON):
         sl_c, sh_c = sigmoid(pl_c), sigmoid(ph_c)
 
-        def coef(r, acc):
+        st = 1 + 2 * it
+
+        def coef(i, acc):
+            r = order(i)
             act = tile(acte, 0, r)
             rest = 1.0 - act
             pc, sc = tile(pre, 0, r), tile(sre, 0, r)
@@ -258,14 +304,8 @@
                 acc = pack(acc, q, k, r)
                 if k < L - 1:
                     pc, sc = pn, sn
+            emit(are, st, i, acc)
             return acc
-
-        def send(ref, st, acc):
-            for e, row in ((0, T), (1, T + NX - 1)):
-                for k in range(L):
-                    srow[st, e, k:k + 1, :] = ref[k, row:row + 1, :]
-                scol[st, e, 0:T, :] = acc[e]
-            start(st, NRL, T)
 
         def apply(ref, k, r, cur, before, after, lo, hi):
             y = plain(dg, k, r) * cur
@@ -279,14 +319,15 @@
                 y = y + plain(ozp, k, r) * after
             return y - shift * cur
 
-        st = 1 + 2 * it
-        acc = lax.fori_loop(0, R, coef, z2)
-        send(are, st, acc)
-        finish(st, NRL, T)
+        lax.fori_loop(0, R, coef, z2)
+        recv(st, 0, NRL)
+        recv(st, 1, T)
         halo_rows(are, st, 0)
-        a_lo, a_hi = rcol[st, 0, 0:T, :], rcol[st, 1, 0:T, :]
-
-        def first(r, c):
+
+        def first(i, c):
+            r = order(i)
+            ready(st, i)
+            a_lo, a_hi = halo(st, i)
             acc, aa, ab, bb = c
             before, cur = None, tile(are, 0, r)
             for k in range(L):
@@ -298,16 +339,19 @@
                 ab = ab + fold(cur * b)
                 bb = bb + fold(b * b)
                 before, cur = cur, after
+            emit(bre, st + 1, i, acc)
             return acc, aa, ab, bb
 
         acc, aa, ab, bb = lax.fori_loop(0, R, first, (z2, zero1, zero1, zero1))
-        send(bre, st + 1, acc)
-        finish(st + 1, NRL, T)
+        recv(st + 1, 0, NRL)
+        recv(st + 1, 1, T)
         halo_rows(bre, st + 1, 0)
-        b_lo, b_hi = rcol[st + 1, 0, 0:T, :], rcol[st + 1, 1, 0:T, :]
         last = it == NEWTON - 1
 
-        def second(r, c):
+        def second(i, c):
+            r = order(i)
+            ready(st + 1, i)
+            b_lo, b_hi = halo(st + 1, i)
             ac, bc, cc = c
             before, cur = None, tile(bre, 0, r)
             for k in range(L):
@@ -390,6 +434,7 @@
                 return c
 
             lax.fori_loop(0, R + 2, step, 0)
+            (a_lo, a_hi), (b_lo, b_hi) = halo(st, R), halo(st + 1, R)
             pl_c = pl_c + (alpha * a_lo + beta * b_lo)
             ph_c = ph_c + (alpha * a_hi + beta * b_hi)
             shift = h11
@@ -404,6 +449,12 @@
                 return c
 
             lax.fori_loop(0, R, end, 0)
+
+    for st, part, n in sent:
+        for to, _, c in copies(st, part, n):
+            @pl.when(to)
+            def _(c=c):
+                c.wait_send()
 
 
 def body(pressure, pressure_old, conductivity, porosity, recharge, active):
@@ -419,15 +470,16 @@
     return pl.pallas_call(
         functools.partial(kernel, L, NX, NY, GX, GY),
         out_shape=(jax.ShapeDtypeStruct(pressure.shape, f32),) * 2,
-        in_specs=[vm] * 6,
+        in_specs=[pl.BlockSpec(memory_space=pl.ANY)] * 6,
         out_specs=(vm, vm),
         scratch_shapes=[ext] * 4 + [cell, pltpu.VMEM((1, NX + 2 * T, NY), f32), cell, cell]
         + [cell] * 5 + [cell] * 7
         + [
-            pltpu.VMEM((ST, 2, NR0, NY), f32), pltpu.VMEM((ST, 2, 3 * T, W), f32),
-            pltpu.VMEM((ST, 2, NR0, NY), f32), pltpu.VMEM((ST, 2, 3 * T, W), f32),
+            pltpu.VMEM((ST, 2, NR0, NY), f32), pltpu.VMEM((ST, 2, 2, 3 * T, W), f32),
+            pltpu.VMEM((ST, 2, NR0, NY), f32), pltpu.VMEM((ST, 2, 2, 3 * T, W), f32),
             pltpu.VMEM((NEWTON, GY, T, W), f32), pltpu.VMEM((NEWTON, GX, T, W), f32),
-            dma((ST, 4)), dma((ST, 4)),
+            pltpu.VMEM((NX, NY), jnp.int32), pltpu.VMEM((NX, NY), f32), dma((6,)),
+            dma((ST, 3, 2)), dma((ST, 3, 2)),
             dma((NEWTON, GY)), dma((NEWTON, GY)), dma((NEWTON, GX)), dma((NEWTON, GX)),
         ],
         compiler_params=pltpu.CompilerParams(

time: 68.1 us -> 56.9 us (0.84)
  Pallas kernels: 63.6 us -> 52.5 us
    pallas_call x1, Pallas kernels: 63.6 us -> 52.5 us  [body(): pl.pallas_call(functools.partial(kernel, L, NX, NY, GX, GY), out_shape=(j...]
where the time goes in v2:
time: 56.9 us; the launch traced here: 56.7 us
  Pallas kernels  52.5 us (92%)
  local copies, waits for them, and re-layouts  3.63 us (6%)
  between operations  0.65 us (1%)
    pallas_call x1, Pallas kernels, body(): pl.pallas_call(functools.partial(kernel, L, NX, NY, GX, GY), out_shape=(j...  52.5 us
    unnamed x4, local copies, waits for them, and re-layouts  3.63 us

profile of v2, /device:TPU:0, one launch (start us, length us, event | category | flops | bytes accessed | tf_op | source)
XLA Modules:
  0.0 56.7 jit_solution(11538883632426523900)
XLA Ops:
  0.6 52.5 %shard_map.77 = (f32[10,64,512]{2,1,0:T(8,128)}, f32[10,64,512]{2,1,0:T(8,128)}) custom-call(f32[10,64,512]{2,1,0:T(8,128)} %p_hbm.1, f32[10,64,512]{2,1,0:T(8,128)} %po_hbm.1, f32[10,64,512]{2,1,0:T(8,128)} %k_hbm.1, f32[10,64,512]{2,1,0:T(8,128)} %por_hbm.1, f32[64,512]{1,0:T(8,128)} %rech_hbm.1, s32[64,512]{1,0:T(8,128)} %act_hbm.1), custom_call_target="tpu_custom_call" | custom-call | tf_op jit(solution)/shard_map/pallas_call | solution.py:470
  53.1 0.0 copy-start
  53.1 2.6 %copy.10 = f32[10,64,512]{2,1,0:T(8,128)} copy(f32[10,64,512]{2,1,0:T(8,128)} %get-tuple-element.4) | data formatting | bytes 2621440
  55.7 0.0 copy-done
  55.7 1.1 %copy.11 = f32[10,64,512]{2,1,0:T(8,128)} copy(f32[10,64,512]{2,1,0:T(8,128)S(1)} %copy-done) | data formatting | bytes 2621440
Async XLA Ops:
  53.1 2.6 %copy-start = (f32[10,64,512]{2,1,0:T(8,128)S(1)}, f32[10,64,512]{2,1,0:T(8,128)}, u32[]{:S(2)}) copy-start(f32[10,64,512]{2,1,0:T(8,128)} %get-tuple-element.5) | copy-start | bytes 3932164

commit v3 on v2

--- a/solution.py
+++ b/solution.py
@@ -30,8 +30,8 @@
 def kernel(
     L, NX, NY, GX, GY,
     p_hbm, po_hbm, k_hbm, por_hbm, rech_hbm, act_hbm,
-    p_out, l_out,
-    pre, sre, are, bre, cre, acte, p9, r0,
+    pre, are, bre, cre, fin,
+    sre, acte, p9, r0,
     txp, txm, typ, tym, tzp,
     dg, oxp, oxm, oyp, oym, ozp, ozm,
     srow, scol, rrow, rcol, sumy, sumx,
@@ -86,7 +86,7 @@
         return jnp.concatenate([v] * (NY // W), axis=1)
 
     def left(cur, halo, k, r):
-        h = pltpu.roll(halo, lax.rem(2 * W - (k * R + r), W), 1)
+        h = pltpu.roll(halo, lax.rem(W + 1 - (k * R + r), W), 1)
         return jnp.where(lane == 0, wide(h), pltpu.roll(cur, 1, 1))
 
     def right(cur, halo, k, r):
@@ -95,9 +95,10 @@
 
     def pack(acc, v, k, r):
         lo, hi = acc
-        at = lane1 == k * R + r
-        lo = jnp.where(at, jnp.broadcast_to(v[:, 0:1], (T, W)), lo)
-        hi = jnp.where(at, jnp.broadcast_to(v[:, NY - 1:NY], (T, W)), hi)
+        both = jnp.where(lane1 == 0, v[:, :W], v[:, NY - W:])
+        both = pltpu.roll(both, k * R + r, 1)
+        lo = jnp.where(lane1 == k * R + r, both, lo)
+        hi = jnp.where(lane1 == lax.rem(k * R + r + W - 1, W), both, hi)
         return lo, hi
 
     zero1 = jnp.zeros((T, W), f32)
@@ -441,20 +442,29 @@
         else:
             ga = 1.0 - w1 * shift - w2 * zf
             gb = w1 + w2 * ze
-            def end(r, c):
-                for k in range(L):
-                    a, b = tile(are, k, r), tile(bre, k, r)
-                    put(p_out, k, r, tile(pre, k, r) + (alpha * a + beta * b))
-                    put(l_out, k, r, ga * a - gb * b - w2 * plain(cre, k, r))
-                return c
-
-            lax.fori_loop(0, R, end, 0)
+            for i, v in enumerate((alpha, beta, ga, gb, w2)):
+                fin[i:i + 1, :] = jnp.broadcast_to(v, (1, W))
 
     for st, part, n in sent:
         for to, _, c in copies(st, part, n):
             @pl.when(to)
             def _(c=c):
                 c.wait_send()
+
+
+def finish_kernel(L, NX, NY, pre, are, bre, cre, fin, p_out, l_out):
+    alpha, beta, ga, gb, w2 = [fin[i:i + 1, 0:1] for i in range(5)]
+    k = pl.program_id(0)
+
+    def end(r, c):
+        at = pl.ds(pl.multiple_of((r + 1) * T, T), T)
+        here = pl.ds(pl.multiple_of(r * T, T), T)
+        a, b = are[k, at, :], bre[k, at, :]
+        p_out[0, here, :] = pre[k, at, :] + (alpha * a + beta * b)
+        l_out[0, here, :] = ga * a - gb * b - w2 * cre[k, here, :]
+        return c
+
+    lax.fori_loop(0, NX // T, end, 0, unroll=True)
 
 
 def body(pressure, pressure_old, conductivity, porosity, recharge, active):
@@ -467,12 +477,12 @@
     NR0 = ((2 * L + 1 + T - 1) // T) * T
     dma = pltpu.SemaphoreType.DMA
     vm = pl.BlockSpec(memory_space=pltpu.VMEM)
-    return pl.pallas_call(
+    mid = pl.pallas_call(
         functools.partial(kernel, L, NX, NY, GX, GY),
-        out_shape=(jax.ShapeDtypeStruct(pressure.shape, f32),) * 2,
-        in_specs=[pl.BlockSpec(memory_space=pl.ANY)] * 6,
-        out_specs=(vm, vm),
-        scratch_shapes=[ext] * 4 + [cell, pltpu.VMEM((1, NX + 2 * T, NY), f32), cell, cell]
+        out_shape=(ext, ext, ext, cell, pltpu.VMEM((T, W), f32)),
+        in_specs=[pl.BlockSpec(memory_space=pltpu.HBM)] * 6,
+        out_specs=(vm,) * 5,
+        scratch_shapes=[ext] + [pltpu.VMEM((1, NX + 2 * T, NY), f32), cell, cell]
         + [cell] * 5 + [cell] * 7
         + [
             pltpu.VMEM((ST, 2, NR0, NY), f32), pltpu.VMEM((ST, 2, 2, 3 * T, W), f32),
@@ -483,9 +493,18 @@
             dma((NEWTON, GY)), dma((NEWTON, GY)), dma((NEWTON, GX)), dma((NEWTON, GX)),
         ],
         compiler_params=pltpu.CompilerParams(
-            collective_id=0, has_side_effects=True, vmem_limit_bytes=64000000
+            collective_id=0, has_side_effects=True, vmem_limit_bytes=60600000
         ),
     )(pressure, pressure_old, conductivity, porosity, recharge, active)
+    block = pl.BlockSpec((1, NX, NY), lambda k: (k, 0, 0))
+    return pl.pallas_call(
+        functools.partial(finish_kernel, L, NX, NY),
+        grid=(L,),
+        out_shape=(jax.ShapeDtypeStruct(pressure.shape, f32),) * 2,
+        in_specs=[vm] * 5,
+        out_specs=(block, block),
+        compiler_params=pltpu.CompilerParams(vmem_limit_bytes=8000000),
+    )(*[pltpu.with_memory_space_constraint(m, pltpu.VMEM) for m in mid])
 
 
 def solution(mesh):

time: 56.9 us -> 54.6 us (0.960)
  local copies, waits for them, and re-layouts: 3.63 us -> 0 us
  Pallas kernels: 52.5 us -> 53.8 us
    unnamed x4 -> x0, local copies, waits for them, and re-layouts: 3.63 us -> none
    pallas_call x1 -> x2, Pallas kernels: 52.5 us -> 53.8 us  [the longest x1 49.9 us: body(): pl.pallas_call(functools.partial(kernel, L, NX, NY, GX, GY), out_shape=(e...]
where the time goes in v3:
time: 54.6 us; the launch traced here: 54.5 us
  Pallas kernels  53.8 us (99%)
  between operations  0.64 us (1%)
    pallas_call x1, Pallas kernels, body(): pl.pallas_call(functools.partial(kernel, L, NX, NY, GX, GY), out_shape=(e...  49.9 us
    pallas_call x1, Pallas kernels, body(): pl.pallas_call(functools.partial(finish_kernel, L, NX, NY), grid=(L,), ou...  3.89 us

profile of v3, /device:TPU:0, one launch (start us, length us, event | category | flops | bytes accessed | tf_op | source)
XLA Modules:
  0.0 54.5 jit_solution(6347544820025392514)
XLA Ops:
  0.6 49.9 %shard_map.77 = (f32[10,80,512]{2,1,0:T(8,128)S(1)}, f32[10,80,512]{2,1,0:T(8,128)S(1)}, f32[10,80,512]{2,1,0:T(8,128)S(1)}, f32[10,64,512]{2,1,0:T(8,128)S(1)}, f32[8,128]{1,0:T(8,128)S(1)}) custom-call(f32[10,64,512]{2,1,0:T(8,128)} %p_hbm.1, f32[10,64,512]{2,1,0:T(8,128)} %po_hbm.1, f32[10,64,512]{2,1,0:T(8,128)} %k_hbm.1, f32[10,64,512]{2,1,0:T(8,128)} %por_hbm.1, ...), custom_call_target="tpu_custom_call" | custom-call | tf_op jit(solution)/shard_map/pallas_call | solution.py:480
  50.6 3.9 %shard_map.78 = (f32[10,64,512]{2,1,0:T(8,128)}, f32[10,64,512]{2,1,0:T(8,128)}) custom-call(f32[10,80,512]{2,1,0:T(8,128)S(1)} %get-tuple-element.7.pre, f32[10,80,512]{2,1,0:T(8,128)S(1)} %get-tuple-element.8.are, f32[10,80,512]{2,1,0:T(8,128)S(1)} %get-tuple-element.9.bre, f32[10,64,512]{2,1,0:T(8,128)S(1)} %get-tuple-element.10.cre, ...), custom_call_target="tpu_custom_call" | custom-call | tf_op jit(solution)/shard_map/pallas_call | solution.py:500

commit v4 on v3

--- a/solution.py
+++ b/solution.py
@@ -62,10 +62,15 @@
     rcol[...] = jnp.zeros_like(rcol)
 
     barrier = pltpu.get_barrier_semaphore()
-    for d in range(1, GX):
-        pl.semaphore_signal(barrier, inc=1, device_id=(lax.rem(gx + d, GX), gy), device_id_type=MESH)
-    for d in range(1, GY):
-        pl.semaphore_signal(barrier, inc=1, device_id=(gx, lax.rem(gy + d, GY)), device_id_type=MESH)
+    ALL = GX * GY <= 32
+    if ALL:
+        greet = [(gx * GY + gy + d) % (GX * GY) for d in range(1, GX * GY)]
+        greet = [(o // GY, lax.rem(o, GY)) for o in greet]
+    else:
+        greet = [(lax.rem(gx + d, GX), gy) for d in range(1, GX)]
+        greet += [(gx, lax.rem(gy + d, GY)) for d in range(1, GY)]
+    for peer in greet:
+        pl.semaphore_signal(barrier, inc=1, device_id=peer, device_id_type=MESH)
 
     def tile(ref, k, r):
         return ref[k, pl.ds(pl.multiple_of((r + 1) * T, T), T), :]
@@ -161,7 +166,7 @@
         scol[0, 0, e, 0:T, :] = pp[e]
         scol[0, 0, e, T:2 * T, :] = kk[e]
         scol[0, 0, e, 2 * T:3 * T, :] = aa[e]
-    pl.semaphore_wait(barrier, GX - 1 + GY - 1)
+    pl.semaphore_wait(barrier, len(greet))
     start(0, 0, NR0)
     start(0, 1, 3 * T)
     for c in loads[3:]:
@@ -257,16 +262,13 @@
 
         def coef(i, acc):
             r = order(i)
-            act = tile(acte, 0, r)
-            rest = 1.0 - act
             pc, sc = tile(pre, 0, r), tile(sre, 0, r)
-            below = None
+            sm = sd = fl = None
             for k in range(L):
                 s2 = sc * sc
                 mc = 0.5 * s2
                 s1 = 1.0 - sc
                 ec = s2 * s1
-                sm = sd = fl = None
                 for pn, sn, tr, off in (
                     (up(pre, k, r, pc), up(sre, k, r, sc), txm, oxm),
                     (down(pre, k, r, pc), down(sre, k, r, sc), txp, oxp),
@@ -283,10 +285,6 @@
                         sm, sd, fl = tm, td, tm * drop
                     else:
                         sm, sd, fl = sm + tm, sd + td, fl + tm * drop
-                if below is not None:
-                    tm, td, f, eb = below
-                    sm, sd, fl = sm + tm, sd - td, fl - f
-                    put(ozm, k, r, -(eb * td + tm))
                 if k < L - 1:
                     pn, sn = tile(pre, k + 1, r), tile(sre, k + 1, r)
                     n2 = sn * sn
@@ -296,15 +294,17 @@
                     td = t * drop
                     f = tm * drop
                     put(ozp, k, r, n2 * (1.0 - sn) * td - tm)
+                    put(ozm, k + 1, r, -(ec * td + tm))
                     sm, sd, fl = sm + tm, sd + td, fl + f
-                    below = (tm, td, f, ec)
                 w = plain(p9, k, r)
+                rest = 1.0 - tile(acte, 0, r)
                 put(dg, k, r, w * sc * s1 + rest + sm + ec * sd)
                 q = plain(r0, k, r) - w * sc - fl - rest * pc
                 put(are, k, r + 1, q)
                 acc = pack(acc, q, k, r)
                 if k < L - 1:
                     pc, sc = pn, sn
+                    sm, sd, fl = tm, -td, -f
             emit(are, st, i, acc)
             return acc
 
@@ -389,9 +389,15 @@
                 tot = tot + buf[it, d]
             return tot
 
-        tot = spread(sumy, GY, gy, lambda o: (gx, o), ysend, yrecv)
-        sumx[it, 0] = tot
-        tot = spread(sumx, GX, gx, lambda o: (o, gy), xsend, xrecv)
+        def flat(o):
+            return (o // GY, lax.rem(o, GY))
+
+        if ALL:
+            tot = spread(sumy, GX * GY, gx * GY + gy, flat, ysend, yrecv)
+        else:
+            tot = spread(sumy, GY, gy, lambda o: (gx, o), ysend, yrecv)
+            sumx[it, 0] = tot
+            tot = spread(sumx, GX, gx, lambda o: (o, gy), xsend, xrecv)
         g = jnp.sum(tot, axis=1, keepdims=True)
         aa, ab, bb, ac, bc, cc = [g[i:i + 1, :] for i in range(6)]
 
@@ -474,6 +480,7 @@
     cell = pltpu.VMEM((L, NX, NY), f32)
     ext = pltpu.VMEM((L, NX + 2 * T, NY), f32)
     ST = 1 + 2 * NEWTON
+    SY = GX * GY if GX * GY <= 32 else GY
     NR0 = ((2 * L + 1 + T - 1) // T) * T
     dma = pltpu.SemaphoreType.DMA
     vm = pl.BlockSpec(memory_space=pltpu.VMEM)
@@ -487,10 +494,10 @@
         + [
             pltpu.VMEM((ST, 2, NR0, NY), f32), pltpu.VMEM((ST, 2, 2, 3 * T, W), f32),
             pltpu.VMEM((ST, 2, NR0, NY), f32), pltpu.VMEM((ST, 2, 2, 3 * T, W), f32),
-            pltpu.VMEM((NEWTON, GY, T, W), f32), pltpu.VMEM((NEWTON, GX, T, W), f32),
+            pltpu.VMEM((NEWTON, SY, T, W), f32), pltpu.VMEM((NEWTON, GX, T, W), f32),
             pltpu.VMEM((NX, NY), jnp.int32), pltpu.VMEM((NX, NY), f32), dma((6,)),
             dma((ST, 3, 2)), dma((ST, 3, 2)),
-            dma((NEWTON, GY)), dma((NEWTON, GY)), dma((NEWTON, GX)), dma((NEWTON, GX)),
+            dma((NEWTON, SY)), dma((NEWTON, SY)), dma((NEWTON, GX)), dma((NEWTON, GX)),
         ],
         compiler_params=pltpu.CompilerParams(
             collective_id=0, has_side_effects=True, vmem_limit_bytes=60600000

time: 54.6 us -> 54.2 us (level)
  no operation moved by 1% of the time
where the time goes in v4:
time: 54.2 us; the launch traced here: 54 us
  Pallas kernels  53.4 us (99%)
  between operations  0.64 us (1%)
    pallas_call x1, Pallas kernels, body(): pl.pallas_call(functools.partial(kernel, L, NX, NY, GX, GY), out_shape=(e...  49.5 us
    pallas_call x1, Pallas kernels, body(): pl.pallas_call(functools.partial(finish_kernel, L, NX, NY), grid=(L,), ou...  3.89 us

profile of v4, /device:TPU:0, one launch (start us, length us, event | category | flops | bytes accessed | tf_op | source)
XLA Modules:
  0.0 54.0 jit_solution(2703608562215366925)
XLA Ops:
  0.6 49.5 %shard_map.77 = (f32[10,80,512]{2,1,0:T(8,128)S(1)}, f32[10,80,512]{2,1,0:T(8,128)S(1)}, f32[10,80,512]{2,1,0:T(8,128)S(1)}, f32[10,64,512]{2,1,0:T(8,128)S(1)}, f32[8,128]{1,0:T(8,128)S(1)}) custom-call(f32[10,64,512]{2,1,0:T(8,128)} %p_hbm.1, f32[10,64,512]{2,1,0:T(8,128)} %po_hbm.1, f32[10,64,512]{2,1,0:T(8,128)} %k_hbm.1, f32[10,64,512]{2,1,0:T(8,128)} %por_hbm.1, ...), custom_call_target="tpu_custom_call" | custom-call | tf_op jit(solution)/shard_map/pallas_call | solution.py:487
  50.1 3.9 %shard_map.78 = (f32[10,64,512]{2,1,0:T(8,128)}, f32[10,64,512]{2,1,0:T(8,128)}) custom-call(f32[10,80,512]{2,1,0:T(8,128)S(1)} %get-tuple-element.7.pre, f32[10,80,512]{2,1,0:T(8,128)S(1)} %get-tuple-element.8.are, f32[10,80,512]{2,1,0:T(8,128)S(1)} %get-tuple-element.9.bre, f32[10,64,512]{2,1,0:T(8,128)S(1)} %get-tuple-element.10.cre, ...), custom_call_target="tpu_custom_call" | custom-call | tf_op jit(solution)/shard_map/pallas_call | solution.py:507
